TPU v7x, 32 devices: a whole 2x2x4 slice. The times are simulated.
32 devices in a mesh: gx: 4 (over z), gy: 2 (over core), gz: 4 (over y, x).
Axes of the slice: x: 2, y: 2, z: 4, core: 2. Of those that a mesh axis runs over, the one named last changes fastest.
Arguments:
- pair: bfloat16 [128, 512, 512], P('gz', 'gx', 'gy'), may hold values from -6 to 6
- pair_mask: int32 [512, 512], P('gx', 'gy'), may hold values from 0 to 1, as said below
- input_gain: float32 [128], replicated, may hold values from 0.1 to 1.9
- input_weights: bfloat16 [4, 128, 128], replicated, may hold values from -0.5 to 0.5
- out_gate_weight: bfloat16 [128, 128], replicated, may hold values from -0.5 to 0.5
- hidden_gain: float32 [128], replicated, may hold values from 0.1 to 1.9
- out_weight: bfloat16 [128, 128], replicated, may hold values from -0.5 to 0.5
Outputs:
- update: bfloat16 [128, 512, 512], P('gz', 'gx', 'gy')
Inputs may be any that keep to these rules, and one draw needn't show every extreme that they name: pair_mask[r, s] = m[r] * m[s] for a 0/1 residue mask m of the draw that is 0 for all r >= L, for one crop length L with 256 < L <= 512; residues below L may also be 0.
All inputs are finite; a program needn't handle non-finite values.
Results may differ from a plain program's by a relative error of at most 0.011.
Values may be sent and summed in bfloat16 or wider, within the bound.
A program may use at most 64 MiB of HBM per device.

v0:
```python
import jax
import jax.numpy as jnp
from jax import lax
from jax.sharding import PartitionSpec as P

EPSILON = 1e-05


def own_columns(matrix, width):
    first = lax.axis_index("gz") * width
    return lax.dynamic_slice_in_dim(matrix, first, width, matrix.ndim - 1)


def gated_sides(weights, normed, mask_values, hidden):
    joined = jnp.concatenate([weights[0], weights[1]], axis=1)
    product = jnp.einsum("dk,drs->krs", joined, normed, preferred_element_type=jnp.float32)
    return (mask_values * jax.nn.sigmoid(product[:hidden]) * product[hidden:]).astype(jnp.bfloat16)


def shards(pair, pair_mask, input_gain, input_weights, out_gate_weight, hidden_gain, out_weight):
    local_channels = pair.shape[0]
    all_channels = input_gain.shape[0]
    all_hidden = hidden_gain.shape[0]
    local_hidden = all_hidden // lax.axis_size("gz")
    mask_values = pair_mask.astype(jnp.float32)
    values = pair.astype(jnp.float32)
    moments = lax.psum((jnp.sum(values, axis=0), jnp.sum(values * values, axis=0)), "gz")
    average = moments[0] / all_channels
    spread = moments[1] / all_channels - average * average
    gains = own_columns(input_gain, local_channels)
    normed_local = ((values - average) * lax.rsqrt(spread + EPSILON) * gains[:, None, None]).astype(
        jnp.bfloat16
    )
    normed = lax.all_gather(normed_local, "gz", axis=0, tiled=True)
    side_weights = own_columns(input_weights, local_hidden)
    left_side = gated_sides(side_weights[0:2], normed, mask_values, local_hidden)
    right_side = gated_sides(side_weights[2:4], normed, mask_values, local_hidden)
    gate_weights = own_columns(out_gate_weight, local_channels)
    gate = jax.nn.sigmoid(
        jnp.einsum("dc,drs->crs", gate_weights, normed, preferred_element_type=jnp.float32)
    )
    left_panels = lax.all_gather(left_side, "gy", axis=2, tiled=True)
    row_blocks = lax.all_to_all(left_panels, "gx", split_axis=2, concat_axis=1, tiled=True)
    triangle = jnp.einsum(
        "cki,ckj->icj",
        row_blocks,
        lax.all_gather(right_side, "gx", axis=1, tiled=True),
        preferred_element_type=jnp.float32,
    )
    hidden_gains = own_columns(hidden_gain, local_hidden)
    hidden_stats = lax.psum((jnp.sum(triangle, axis=1), jnp.sum(triangle * triangle, axis=1)), "gz")
    hidden_mean = hidden_stats[0] / all_hidden
    hidden_spread = hidden_stats[1] / all_hidden - hidden_mean * hidden_mean
    hidden_normed = (
        (triangle - hidden_mean[:, None, :])
        * lax.rsqrt(hidden_spread + EPSILON)[:, None, :]
        * hidden_gains[None, :, None]
    ).astype(jnp.bfloat16)
    every_hidden = lax.all_gather(hidden_normed, "gz", axis=1, tiled=True)
    out_columns = own_columns(out_weight, local_channels)
    projected = jnp.einsum(
        "hc,ihj->cij", out_columns, every_hidden, preferred_element_type=jnp.float32
    )
    return (mask_values * gate * projected).astype(jnp.bfloat16)


def solution(mesh):
    placed = (P("gz", "gx", "gy"), P("gx", "gy"), P(), P(), P(), P(), P())
    return jax.shard_map(
        shards, mesh=mesh, in_specs=placed, out_specs=P("gz", "gx", "gy"), check_vma=False
    )
```

profile of v0, /device:TPU:26, one launch (start us, length us, event | category | flops | bytes accessed | tf_op | source)
XLA Modules:
  0.0 591.4 jit_solution(12267018574907195706)
XLA Ops:
  6.5 4.8 convert_reduce_fusion
  11.4 0.8 dynamic_slice.16
  12.2 43.4 %all-reduce.7.cloned.1.call-done = (f32[128,256]{1,0:T(8,128)}, f32[128,256]{1,0:T(8,128)}) async-done(((f32[128,256]{1,0:T(8,128)}, f32[128,256]{1,0:T(8,128)}), (f32[128,256]{1,0:T(8,128)}, f32[128,256]{1,0:T(8,128)})) %all-reduce.7.cloned.1.call-update) | async-done | bytes 262160 | tf_op jit(solution)/shard_map/psum | solution.py:27
  55.5 1.0 broadcast_multiply_fusion.1
  56.6 3.0 fusion.6
  60.2 87.1 %all-gather.5.cloned.1.call-done = bf16[128,128,256]{2,0,1:T(8,128)(2,1)} async-done(((bf16[32,128,256]{2,0,1:T(8,128)(2,1)}), bf16[128,128,256]{2,0,1:T(8,128)(2,1)}) %all-gather.5.cloned.1.call-update) | async-done | bytes 8388624 | tf_op jit(solution)/shard_map/all_gather | solution.py:34
  147.2 4.8 fusion.29
  152.1 1.0 slice-done.1
  153.1 1.3 fusion.26
  154.4 4.1 fusion.13
  159.1 12.6 %all-gather.9.cloned.1.call-done = bf16[32,128,512]{2,0,1:T(8,128)(2,1)} async-done(((bf16[32,128,256]{2,0,1:T(8,128)(2,1)}), bf16[32,128,512]{2,0,1:T(8,128)(2,1)}) %all-gather.9.cloned.1.call-update) | async-done | bytes 4194320 | tf_op jit(solution)/shard_map/all_gather | solution.py:42
  171.7 9.2 %copy.34 = bf16[32,128,512]{1,0,2:T(8,128)(2,1)} copy(bf16[32,128,512]{2,0,1:T(8,128)(2,1)} %all-gather.9.cloned.1.call-done) | data formatting | bytes 8388608 | tf_op jit(solution)/shard_map/all_gather | solution.py:42
  180.9 206.9 %all_to_all.18 = bf16[32,128,512]{1,0,2:T(8,128)(2,1)} all-to-all(bf16[32,128,512]{1,0,2:T(8,128)(2,1)} %copy.34), channel_id=1, replica_groups=mesh['gx'=4,'gy'=2,'gz'=4] {'gx'}, dimensions={2} | all-to-all | bytes 8388608 | tf_op jit(solution)/shard_map/all_to_all | solution.py:43
  387.8 7.6 %copy.35 = bf16[32,128,4,128]{3,1,2,0:T(8,128)(2,1)} copy(bf16[32,128,4,128]{1,0,3,2:T(8,128)(2,1)} %bitcast.40) | data formatting | bytes 8388608 | tf_op jit(solution)/shard_map/all_to_all | solution.py:43
  395.4 14.8 %all-gather.7.cloned.1.call-done = bf16[32,512,256]{2,0,1:T(8,128)(2,1)} async-done(((bf16[32,128,256]{2,0,1:T(8,128)(2,1)}), bf16[32,512,256]{2,0,1:T(8,128)(2,1)}) %all-gather.7.cloned.1.call-update) | async-done | bytes 8388624 | tf_op jit(solution)/shard_map/all_gather | solution.py:47
  410.2 17.5 %bitcast_reduce_fusion = (f32[128,256]{0,1:T(8,128)S(1)}, f32[128,256]{0,1:T(8,128)S(1)}, f32[32,256,128]{2,1,0:T(8,128)}) fusion(bf16[32,512,128]{2,1,0:T(8,128)(2,1)} %bitcast.41, bf16[32,512,256]{2,0,1:T(8,128)(2,1)} %all-gather.7.cloned.1.call-done), kind=kOutput, calls=%fused_computation.27 | convolution fusion | flops 1076822016 | bytes 17039360 | tf_op jit(solution)/shard_map/cki,ckj->icj/dot_general | solution.py:44
  429.7 43.9 %all-reduce.5.cloned.1.call-done = (f32[128,256]{1,0:T(8,128)}, f32[128,256]{1,0:T(8,128)}) async-done(((f32[128,256]{1,0:T(8,128)}, f32[128,256]{1,0:T(8,128)}), (f32[128,256]{1,0:T(8,128)}, f32[128,256]{1,0:T(8,128)})) %all-reduce.5.cloned.1.call-update) | async-done | bytes 262160 | tf_op jit(solution)/shard_map/psum | solution.py:51
  473.5 1.0 broadcast_multiply_fusion
  474.8 2.9 fusion.20
  477.7 2.9 copy.41
  480.6 87.6 %all-gather.11.cloned.1.call-done = bf16[128,128,256]{2,0,1:T(8,128)(2,1)} async-done(((bf16[128,32,256]{2,0,1:T(8,128)(2,1)}), bf16[128,128,256]{2,0,1:T(8,128)(2,1)}) %all-gather.11.cloned.1.call-update) | async-done | bytes 8388624 | tf_op jit(solution)/shard_map/all_gather | solution.py:59
  568.2 8.7 %fusion = f32[32,128,256]{2,0,1:T(8,128)S(1)} fusion(bf16[128,128,256]{2,0,1:T(8,128)(2,1)} %all-gather.11.cloned.1.call-done, bf16[128,128]{1,0:T(8,128)(2,1)S(1)} %copy-done, s32[]{:T(128)S(6)} %select_n.2), kind=kOutput, calls=%fused_computation | convolution fusion | flops 268435456 | bytes 12615684 | tf_op jit(solution)/shard_map/hc,ihj->cij/dot_general | solution.py:61
  576.9 5.1 multiply_convert_fusion
  582.1 2.5 copy.43
  (39 shorter events, 3.3 us)
Async XLA Ops:
  6.5 561.7 %copy-start = (bf16[128,128]{1,0:T(8,128)(2,1)S(1)}, bf16[128,128]{1,0:T(8,128)(2,1)}, u32[]{:S(2)}) copy-start(bf16[128,128]{1,0:T(8,128)(2,1)} %param.13) | copy-start | bytes 98308
  6.5 50.0 %copy-start.1 = (bf16[32,128,256]{2,1,0:T(8,128)(2,1)S(1)}, bf16[32,128,256]{2,1,0:T(8,128)(2,1)}, u32[]{:S(2)}) copy-start(bf16[32,128,256]{2,1,0:T(8,128)(2,1)} %param.7) | copy-start | bytes 6291460
  6.5 49.0 %all-reduce.7.cloned.1.call-start = ((), (), s32[]{:S(2)}) async-start(), calls=%async_computation.6 | async-start | bytes 524288 | tf_op jit(solution)/shard_map/psum | solution.py:27
  11.3 48.3 %copy-start.2 = (bf16[4,128,128]{2,1,0:T(8,128)(2,1)S(1)}, bf16[4,128,128]{2,1,0:T(8,128)(2,1)}, u32[]{:S(2)}) copy-start(bf16[4,128,128]{2,1,0:T(8,128)(2,1)} %param.10) | copy-start | bytes 393220
  11.3 48.8 %copy-start.3 = (s32[128,256]{1,0:T(8,128)S(1)}, s32[128,256]{1,0:T(8,128)}, u32[]{:S(2)}) copy-start(s32[128,256]{1,0:T(8,128)} %param.8) | copy-start | bytes 393220
  11.3 135.9 %all-gather.5.cloned.1.call-start = ((), (), s32[]{:S(2)}) async-start(), calls=%async_computation.1 | async-start | bytes 10485760 | tf_op jit(solution)/shard_map/all_gather | solution.py:34
  59.6 112.1 %all-gather.9.cloned.1.call-start = ((), (), s32[]{:S(2)}) async-start(), calls=%async_computation.3 | async-start | bytes 6291456 | tf_op jit(solution)/shard_map/all_gather | solution.py:42
  147.2 4.8 slice-start
  147.2 5.9 slice-start.1
  158.5 251.8 %all-gather.7.cloned.1.call-start = ((), (), s32[]{:S(2)}) async-start(), calls=%async_computation.2 | async-start | bytes 10485760 | tf_op jit(solution)/shard_map/all_gather | solution.py:47
  159.1 314.5 %all-reduce.5.cloned.1.call-start = ((), (), s32[]{:S(2)}) async-start(), calls=%async_computation.5 | async-start | bytes 524288 | tf_op jit(solution)/shard_map/psum | solution.py:51
  410.2 19.4 %copy-start.5 = (f32[128]{0:T(128)S(1)}, f32[128]{0:T(128)}, u32[]{:S(2)}) copy-start(f32[128]{0:T(128)} %param.12) | copy-start | bytes 1540
  429.3 138.9 %all-gather.11.cloned.1.call-start = ((), (), s32[]{:S(2)}) async-start(), calls=%async_computation.4 | async-start | bytes 10485760 | tf_op jit(solution)/shard_map/all_gather | solution.py:59
  480.6 96.3 %copy-start.4 = (bf16[128,128]{1,0:T(8,128)(2,1)S(1)}, bf16[128,128]{1,0:T(8,128)(2,1)}, u32[]{:S(2)}) copy-start(bf16[128,128]{1,0:T(8,128)(2,1)} %param.11) | copy-start | bytes 98308
Sparse Core Ops, SparseCore 0:
  11.5 44.0 all-reduce.6
  59.7 87.4 all-gather.4
  158.6 13.0 all-gather.8
  173.1 237.0 all-gather.6
  429.4 44.0 all-reduce.4
  480.7 87.4 all-gather.10
where the time goes:
time: 594 us; the launch traced here: 591 us
  waiting for transfers between devices  290 us (49%)
  blocking collectives  207 us (35%)
  matrix products  37.5 us (6%)
  local copies, waits for them, and re-layouts  26.2 us (4%)
  other arithmetic  16.8 us (3%)
  between operations  13.6 us (2%)
    all_to_all x1, blocking collectives, shards(): lax.all_to_all(left_panels, 'gx', split_axis=2, concat_axis=1, tiled=True)  207 us
    all_gather x1, waiting for transfers between devices, shards(): every_hidden = lax.all_gather(hidden_normed, 'gz', axis=1, tiled=True)  87.6 us
    all_gather x1, waiting for transfers between devices, shards(): normed = lax.all_gather(normed_local, 'gz', axis=0, tiled=True)  87.1 us
    psum x1, waiting for transfers between devices, shards(): lax.psum((jnp.sum(triangle, axis=1), jnp.sum(triangle * triangle, axis=1)...  43.9 us
    psum x1, waiting for transfers between devices, shards(): lax.psum((jnp.sum(values, axis=0), jnp.sum(values * values, axis=0)), 'gz')  43.4 us
    dot_general x1, matrix products, shards(): jnp.einsum('cki,ckj->icj', row_blocks, lax.all_gather(right_side, 'gx', a...  17.5 us
    all_gather x1, waiting for transfers between devices, shards(): lax.all_gather(right_side, 'gx', axis=1, tiled=True)  14.8 us
    all_gather x1, waiting for transfers between devices, shards(): left_panels = lax.all_gather(left_side, 'gy', axis=2, tiled=True)  12.6 us
  transfers between devices with their start and end apart: 6, of which 6 were waited for; matrix products, arithmetic and copies ran while one was open for 3% of the time, Pallas kernels for 0%

commit v1 on v0

v1 whole, which is shorter than its diff:
```python
import functools

import jax
import jax.numpy as jnp
from jax import lax
from jax.experimental import pallas as pl
from jax.experimental.pallas import tpu as pltpu
from jax.sharding import PartitionSpec as P

EPSILON = 1e-05
MESH = pl.DeviceIdType.MESH


def position(axes):
    at = 0
    for name in axes:
        at = at * lax.axis_size(name) + lax.axis_index(name)
    return at


def coordinates(axes, at):
    where = {}
    for name in reversed(axes):
        where[name] = lax.rem(at, lax.axis_size(name))
        at = at // lax.axis_size(name)
    return where


def block(ref, axis, at, width):
    cut = [slice(None)] * len(ref.shape)
    cut[axis] = pl.ds(pl.multiple_of(at * width, width), width)
    return ref.at[tuple(cut)]


def greet(axes, others):
    me = position(axes)
    barrier = pltpu.get_barrier_semaphore()

    @pl.loop(1, others + 1)
    def _(step):
        there = coordinates(axes, lax.rem(me + step, others + 1))
        pl.semaphore_signal(barrier, inc=1, device_id=there, device_id_type=MESH)

    pl.semaphore_wait(barrier, others)


def exchange_kernel(axes, split, concat, count, src, dst, held, sends, receives, own):
    me = position(axes)
    wide = src.shape[split] // count
    tall = src.shape[concat]
    greet(axes, count - 1)

    def copy(step, sender, target):
        return pltpu.make_async_remote_copy(
            src_ref=block(src, split, target, wide),
            dst_ref=block(dst, concat, sender, tall),
            send_sem=sends.at[step],
            recv_sem=receives.at[step],
            device_id=coordinates(axes, target),
            device_id_type=MESH,
        )

    @pl.loop(1, count)
    def _(step):
        copy(step, me, lax.rem(me + step, count)).start()

    inward = pltpu.make_async_copy(block(src, split, me, wide), held, own)
    inward.start()
    inward.wait()
    outward = pltpu.make_async_copy(held, block(dst, concat, me, tall), own)
    outward.start()
    outward.wait()

    @pl.loop(1, count)
    def _(step):
        copy(step, lax.rem(me - step + count, count), lax.rem(me + step, count)).wait()


def exchange(value, axes, split, concat, number):
    count = 1
    for name in axes:
        count = count * lax.axis_size(name)
    shape = list(value.shape)
    shape[split] //= count
    piece = tuple(shape)
    shape[concat] *= count
    return pl.pallas_call(
        functools.partial(exchange_kernel, axes, split, concat, count),
        out_shape=jax.ShapeDtypeStruct(tuple(shape), value.dtype),
        in_specs=[pl.BlockSpec(memory_space=pl.ANY)],
        out_specs=pl.BlockSpec(memory_space=pl.ANY),
        scratch_shapes=[
            pltpu.VMEM(piece, value.dtype),
            pltpu.SemaphoreType.DMA((count,)),
            pltpu.SemaphoreType.DMA((count,)),
            pltpu.SemaphoreType.DMA,
        ],
        compiler_params=pltpu.CompilerParams(collective_id=number, has_side_effects=True),
    )(value)


def pair_exchange_kernel(axes, count, left, right, wide_left, far_right, held, sends, receives, gsend, greceive, own):
    me = position(axes)
    core = lax.axis_index("gy")
    cores = lax.axis_size("gy")
    hidden, tall, span = left.shape
    depth = hidden // count
    barrier = pltpu.get_barrier_semaphore()

    @pl.loop(1, count)
    def _(step):
        there = coordinates(axes, lax.rem(me + step, count))
        pl.semaphore_signal(barrier, inc=1, device_id=there, device_id_type=MESH)

    for ahead in range(1, cores):
        pl.semaphore_signal(
            barrier, inc=1, device_id={"gy": lax.rem(core + ahead, cores)}, device_id_type=MESH
        )
    pl.semaphore_wait(barrier, count - 1 + cores - 1)
    columns = pl.ds(pl.multiple_of(core * span, span), span)

    def landing(side, sender):
        rows = pl.ds(pl.multiple_of(sender * tall, tall), tall)
        return wide_left.at[:, rows, columns] if side == 0 else far_right.at[:, rows, :]

    def copy(side, step, sender, target):
        return pltpu.make_async_remote_copy(
            src_ref=block((left, right)[side], 0, target, depth),
            dst_ref=landing(side, sender),
            send_sem=sends.at[side, step],
            recv_sem=receives.at[side, step],
            device_id=coordinates(axes, target),
            device_id_type=MESH,
        )

    for side in range(2):
        @pl.loop(1, count)
        def _(step):
            copy(side, step, me, lax.rem(me + step, count)).start()

    for side in range(2):
        inward = pltpu.make_async_copy(block((left, right)[side], 0, me, depth), held, own)
        inward.start()
        inward.wait()
        outward = pltpu.make_async_copy(held, landing(side, me), own)
        outward.start()
        outward.wait()

    @pl.loop(1, count)
    def _(step):
        copy(0, step, lax.rem(me - step + count, count), lax.rem(me + step, count)).wait()

    passes = [
        pltpu.make_async_remote_copy(
            src_ref=wide_left.at[:, :, columns],
            dst_ref=wide_left.at[:, :, columns],
            send_sem=gsend.at[ahead],
            recv_sem=greceive.at[ahead],
            device_id={"gy": lax.rem(core + ahead, cores)},
            device_id_type=MESH,
        )
        for ahead in range(1, cores)
    ]
    for one in passes:
        one.start()

    @pl.loop(1, count)
    def _(step):
        copy(1, step, lax.rem(me - step + count, count), lax.rem(me + step, count)).wait()

    for one in passes:
        one.wait()


def pair_exchange(left, right, axes, number):
    count = 1
    for name in axes:
        count = count * lax.axis_size(name)
    cores = lax.axis_size("gy")
    hidden, tall, span = left.shape
    depth = hidden // count
    return pl.pallas_call(
        functools.partial(pair_exchange_kernel, axes, count),
        out_shape=(
            jax.ShapeDtypeStruct((depth, tall * count, span * cores), left.dtype),
            jax.ShapeDtypeStruct((depth, tall * count, span), left.dtype),
        ),
        in_specs=[pl.BlockSpec(memory_space=pl.ANY)] * 2,
        out_specs=(pl.BlockSpec(memory_space=pl.ANY),) * 2,
        scratch_shapes=[
            pltpu.VMEM((depth, tall, span), left.dtype),
            pltpu.SemaphoreType.DMA((2, count)),
            pltpu.SemaphoreType.DMA((2, count)),
            pltpu.SemaphoreType.DMA((cores,)),
            pltpu.SemaphoreType.DMA((cores,)),
            pltpu.SemaphoreType.DMA,
        ],
        compiler_params=pltpu.CompilerParams(collective_id=number, has_side_effects=True),
    )(left, right)


def layer_norm(values, gains):
    average = jnp.mean(values, axis=0)
    spread = jnp.mean(jnp.square(values - average), axis=0)
    return ((values - average) * lax.rsqrt(spread + EPSILON) * gains[:, None, None]).astype(jnp.bfloat16)


def project(weights, normed):
    return jnp.einsum("dk,drs->krs", weights, normed, preferred_element_type=jnp.float32)


def shards(pair, pair_mask, input_gain, input_weights, out_gate_weight, hidden_gain, out_weight):
    flat = ("gx", "gz")
    rows = pair.shape[1] // lax.axis_size("gz")
    own_mask = lax.dynamic_slice_in_dim(pair_mask, lax.axis_index("gz") * rows, rows, 0)
    mask_values = own_mask.astype(jnp.float32)
    every_channel = exchange(pair, ("gz",), 1, 0, 0)
    normed = layer_norm(every_channel.astype(jnp.float32), input_gain)
    left, right = (
        (
            mask_values
            * jax.nn.sigmoid(project(input_weights[at], normed))
            * project(input_weights[at + 1], normed)
        ).astype(jnp.bfloat16)
        for at in (0, 2)
    )
    gate = jax.nn.sigmoid(project(out_gate_weight, normed))
    wide_left, far_right = pair_exchange(left, right, flat, 1)
    triangle = jnp.einsum(
        "hki,hkj->hij", wide_left, far_right, preferred_element_type=jnp.float32
    ).astype(jnp.bfloat16)
    every_hidden = exchange(triangle, flat, 1, 0, 2)
    hidden_normed = layer_norm(every_hidden.astype(jnp.float32), hidden_gain)
    projected = project(out_weight, hidden_normed)
    update = (mask_values * gate * projected).astype(jnp.bfloat16)
    return exchange(update, ("gz",), 0, 1, 3)


def solution(mesh):
    placed = (P("gz", "gx", "gy"), P("gx", "gy"), P(), P(), P(), P(), P())
    return jax.shard_map(
        shards, mesh=mesh, in_specs=placed, out_specs=P("gz", "gx", "gy"), check_vma=False
    )
```

time: 594 us -> 295 us (0.50)
  waiting for transfers between devices: 290 us -> 0 us
  blocking collectives: 207 us -> 0 us
  Pallas kernels: 0 us -> 201 us
  matrix products: 37.5 us -> 23.4 us
  between operations: 13.6 us -> 0.15 us
  local copies, waits for them, and re-layouts: 26.2 us -> 39.6 us
  other arithmetic: 16.8 us -> 27 us
    all_to_all x1 -> x0, blocking collectives: 207 us -> none  [shards(): lax.all_to_all(left_panels, 'gx', split_axis=2, concat_axis=1, tiled=True)]
    all_gather x4 -> x0, waiting for transfers between devices: 202 us -> none  [the longest x1 87.6 us: shards(): every_hidden = lax.all_gather(hidden_normed, 'gz', axis=1, tiled=True)]
    pallas_call x0 -> x4, Pallas kernels: none -> 201 us  [the longest x3 109 us: exchange(): pl.pallas_call(functools.partial(exchange_kernel, axes, split, concat, co...]
    psum x2 -> x0, waiting for transfers between devices: 87.2 us -> none  [the longest x1 43.9 us: shards(): lax.psum((jnp.sum(triangle, axis=1), jnp.sum(triangle * triangle, axis=1)...]
    dot_general x0 -> x6, local copies, waits for them, and re-layouts: none -> 33 us  [project(): jnp.einsum('dk,drs->krs', weights, normed, preferred_element_type=jnp.flo...]
    dot_general x5 -> x7, matrix products: 37.5 us -> 23.4 us  [the longest x6 17.7 us: project(): jnp.einsum('dk,drs->krs', weights, normed, preferred_element_type=jnp.flo...]
    all_gather x1 -> x0, local copies, waits for them, and re-layouts: 9.18 us -> none  [shards(): left_panels = lax.all_gather(left_side, 'gy', axis=2, tiled=True)]
    convert_element_type x4 -> x5, other arithmetic: 10 us -> 18.3 us  [the longest x1 8.93 us: shards(): left, right = ((mask_values * jax.nn.sigmoid(project(input_weights[at], n...]
  transfers between devices with their start and end apart: 6 -> 0, of which waited for: 6 -> 0; matrix products, arithmetic and copies ran while one was open for 3% -> 0% of each run, Pallas kernels for 0% -> 0%
where the time goes in v1:
time: 295 us; the launch traced here: 291 us
  Pallas kernels  201 us (68%)
  local copies, waits for them, and re-layouts  39.6 us (13%)
  other arithmetic  27 us (9%)
  matrix products  23.4 us (8%)
    pallas_call x3, Pallas kernels, exchange(): pl.pallas_call(functools.partial(exchange_kernel, axes, split, concat, co...  109 us
    pallas_call x1, Pallas kernels, pair_exchange(): pl.pallas_call(functools.partial(pair_exchange_kernel, axes, count), out_...  92.5 us
    dot_general x6, local copies, waits for them, and re-layouts, project(): jnp.einsum('dk,drs->krs', weights, normed, preferred_element_type=jnp.flo...  33 us
    dot_general x6, matrix products, project(): jnp.einsum('dk,drs->krs', weights, normed, preferred_element_type=jnp.flo...  17.7 us
    convert_element_type x1, other arithmetic, shards(): left, right = ((mask_values * jax.nn.sigmoid(project(input_weights[at], n...  8.93 us
    convert_element_type x1, other arithmetic, shards(): update = (mask_values * gate * projected).astype(jnp.bfloat16)  6.06 us

profile of v1, /device:TPU:26, one launch (start us, length us, event | category | flops | bytes accessed | tf_op | source)
XLA Modules:
  0.0 291.3 jit_solution(1150311163048763597)
XLA Ops:
  0.8 26.3 %shard_map.73 = bf16[128,32,256]{2,1,0:T(8,128)(2,1)} custom-call(bf16[32,128,256]{2,1,0:T(8,128)(2,1)} %src.1), custom_call_target="tpu_custom_call" | custom-call | tf_op jit(solution)/shard_map/pallas_call | solution.py:87
  27.0 2.1 convert_reduce_fusion.1
  29.2 2.2 fusion.7
  33.3 3.4 %copy.8 = bf16[128,32,256]{0,2,1:T(8,128)(2,1)S(1)} copy(bf16[128,32,256]{2,1,0:T(8,128)(2,1)} %fusion.9) | data formatting | bytes 4194304 | tf_op jit(solution)/shard_map/convert_element_type | solution.py:205
  36.8 2.7 fusion.16
  39.5 5.5 %copy.17 = f32[32,256,128]{1,0,2:T(8,128)} copy(f32[32,256,128]{2,1,0:T(8,128)} %fusion.16) | data formatting | bytes 8388608 | tf_op jit(solution)/shard_map/dk,drs->krs/dot_general | solution.py:209
  45.0 2.7 fusion.18
  47.6 5.5 %copy.15 = f32[32,256,128]{1,0,2:T(8,128)} copy(f32[32,256,128]{2,1,0:T(8,128)} %fusion.18) | data formatting | bytes 8388608 | tf_op jit(solution)/shard_map/dk,drs->krs/dot_general | solution.py:209
  53.1 2.6 fusion.20
  55.8 5.5 %copy.13 = f32[32,256,128]{1,0,2:T(8,128)} copy(f32[32,256,128]{2,1,0:T(8,128)} %fusion.20) | data formatting | bytes 8388608 | tf_op jit(solution)/shard_map/dk,drs->krs/dot_general | solution.py:209
  61.3 2.6 fusion.22
  63.9 5.5 %copy.11 = f32[32,256,128]{1,0,2:T(8,128)} copy(f32[32,256,128]{2,1,0:T(8,128)} %fusion.22) | data formatting | bytes 8388608 | tf_op jit(solution)/shard_map/dk,drs->krs/dot_general | solution.py:209
  69.4 8.9 %fusion.13 = (bf16[128,32,256]{2,1,0:T(8,128)(2,1)}, bf16[128,32,256]{2,1,0:T(8,128)(2,1)}) fusion(f32[32,256,128]{1,0,2:T(8,128)} %copy.17, f32[32,256,128]{1,0,2:T(8,128)} %copy.15, f32[32,256]{1,0:T(8,128)S(1)} %dynamic-slice_convert_fusion, f32[32,256,128]{1,0,2:T(8,128)} %copy.13, f32[32,256,128]{1,0,2:T(8,128)} %copy.11), kind=kLoop, calls=%fused_computation.20 | loop fusion | flops 12582912 | bytes 21004288 | tf_op jit(solution)/shard_map/convert_element_type | solution.py:224
  78.3 2.7 fusion.24
  81.0 5.5 %copy.9 = f32[32,256,128]{1,0,2:T(8,128)} copy(f32[32,256,128]{2,1,0:T(8,128)} %fusion.24) | data formatting | bytes 8388608 | tf_op jit(solution)/shard_map/dk,drs->krs/dot_general | solution.py:209
  86.5 92.5 %shard_map.74 = (bf16[8,512,512]{2,1,0:T(8,128)(2,1)}, bf16[8,512,256]{2,1,0:T(8,128)(2,1)}) custom-call(bf16[128,32,256]{2,1,0:T(8,128)(2,1)} %get-tuple-element.10.left, bf16[128,32,256]{2,1,0:T(8,128)(2,1)} %get-tuple-element.9.right), custom_call_target="tpu_custom_call" | custom-call | tf_op jit(solution)/shard_map/pallas_call | solution.py:182
  179.0 5.6 %convolution_convert_fusion.src = bf16[8,512,256]{2,1,0:T(8,128)(2,1)} fusion(bf16[8,512,512]{2,1,0:T(8,128)(2,1)} %get-tuple-element.7, bf16[8,512,256]{2,1,0:T(8,128)(2,1)} %get-tuple-element.8), kind=kOutput, calls=%fused_computation.22 | convolution fusion | flops 1074790400 | bytes 8388608 | tf_op jit(solution)/shard_map/hki,hkj->hij/dot_general | solution.py:229
  184.6 53.0 %shard_map.75 = bf16[128,32,256]{2,1,0:T(8,128)(2,1)} custom-call(bf16[8,512,256]{2,1,0:T(8,128)(2,1)} %convolution_convert_fusion.src), custom_call_target="tpu_custom_call" | custom-call | tf_op jit(solution)/shard_map/pallas_call | solution.py:87
  239.8 2.2 fusion.4
  242.6 4.5 %fusion.10 = f32[32,256,128]{2,1,0:T(8,128)} fusion(bf16[128,32,256]{2,1,0:T(8,128)(2,1)S(1)} %fusion.6, bf16[128,128]{1,0:T(8,128)(2,1)S(1)} %copy-done.4), kind=kOutput, calls=%fused_computation.17 | convolution fusion | flops 268435456 | bytes 6324224 | tf_op jit(solution)/shard_map/dk,drs->krs/dot_general | solution.py:209
  247.1 5.5 %copy.20 = f32[32,256,128]{1,0,2:T(8,128)} copy(f32[32,256,128]{2,1,0:T(8,128)} %fusion.10) | data formatting | bytes 8388608 | tf_op jit(solution)/shard_map/dk,drs->krs/dot_general | solution.py:209
  252.6 6.1 %fusion.14.src = bf16[128,32,256]{2,1,0:T(8,128)(2,1)} fusion(f32[32,256,128]{1,0,2:T(8,128)} %copy.20, f32[32,256,128]{1,0,2:T(8,128)} %copy.9, f32[32,256]{1,0:T(8,128)S(1)} %dynamic-slice_convert_fusion), kind=kLoop, calls=%fused_computation.21 | loop fusion | flops 6291456 | bytes 10518528 | tf_op jit(solution)/shard_map/convert_element_type | solution.py:235
  258.7 29.5 %shard_map.76 = bf16[32,128,256]{2,1,0:T(8,128)(2,1)} custom-call(bf16[128,32,256]{2,1,0:T(8,128)(2,1)} %fusion.14.src), custom_call_target="tpu_custom_call" | custom-call | tf_op jit(solution)/shard_map/pallas_call | solution.py:87
  288.2 3.1 %copy.25 = bf16[32,128,256]{2,1,0:T(8,128)(2,1)} copy(bf16[32,128,256]{2,1,0:T(8,128)(2,1)} %shard_map.76) | data formatting | bytes 4194304
  (22 shorter events, 5.5 us)
Async XLA Ops:
  0.0 78.3 %copy-start = (bf16[128,128]{1,0:T(8,128)(2,1)S(1)}, bf16[128,128]{1,0:T(8,128)(2,1)}, u32[]{:S(2)}) copy-start(bf16[128,128]{1,0:T(8,128)(2,1)} %param.11) | copy-start | bytes 98308
  0.8 30.6 %copy-start.5 = (f32[128]{0:T(128)S(1)}, f32[128]{0:T(128)}, u32[]{:S(2)}) copy-start(f32[128]{0:T(128)} %param.9) | copy-start | bytes 1540
  27.0 4.3 %copy-start.2 = (bf16[128,32,256]{2,1,0:T(8,128)(2,1)S(1)}, bf16[128,32,256]{2,1,0:T(8,128)(2,1)}, u32[]{:S(2)}) copy-start(bf16[128,32,256]{2,1,0:T(8,128)(2,1)} %shard_map.73) | copy-start | bytes 6291460
  31.4 5.4 %copy-start.3 = (bf16[4,128,128]{2,1,0:T(8,128)(2,1)S(1)}, bf16[4,128,128]{2,1,0:T(8,128)(2,1)}, u32[]{:S(2)}) copy-start(bf16[4,128,128]{2,1,0:T(8,128)(2,1)} %param.10) | copy-start | bytes 393220
  184.6 57.3 %copy-start.6 = (f32[128]{0:T(128)S(1)}, f32[128]{0:T(128)}, u32[]{:S(2)}) copy-start(f32[128]{0:T(128)} %param.12) | copy-start | bytes 1540
  237.6 4.3 %copy-start.1 = (bf16[128,32,256]{2,1,0:T(8,128)(2,1)S(1)}, bf16[128,32,256]{2,1,0:T(8,128)(2,1)}, u32[]{:S(2)}) copy-start(bf16[128,32,256]{2,1,0:T(8,128)(2,1)} %shard_map.75) | copy-start | bytes 6291460
  237.6 5.0 %copy-start.4 = (bf16[128,128]{1,0:T(8,128)(2,1)S(1)}, bf16[128,128]{1,0:T(8,128)(2,1)}, u32[]{:S(2)}) copy-start(bf16[128,128]{1,0:T(8,128)(2,1)} %param.13) | copy-start | bytes 98308

commit v2 on v0

v2 whole, which is shorter than its diff:
```python
import functools

import jax
import jax.numpy as jnp
from jax import lax
from jax.experimental import pallas as pl
from jax.experimental.pallas import tpu as pltpu
from jax.sharding import PartitionSpec as P

EPSILON = 1e-05
MESH = pl.DeviceIdType.MESH


def position(axes):
    at = 0
    for name in axes:
        at = at * lax.axis_size(name) + lax.axis_index(name)
    return at


def coordinates(axes, at):
    where = {}
    for name in reversed(axes):
        where[name] = lax.rem(at, lax.axis_size(name))
        at = at // lax.axis_size(name)
    return where


ROWS = 8
LANES = 128


def panels(span):
    return [(at, slice(at * LANES, (at + 1) * LANES)) for at in range(span // LANES)]


def row_of(store, row, height, span):
    parts = [store[at, pl.ds(row, height, stride=ROWS), :] for at, _ in panels(span)]
    return jnp.concatenate(parts, axis=1)


def put_row(store, row, height, span, value):
    for at, lanes in panels(span):
        store[at, pl.ds(row, height, stride=ROWS), :] = value[:, lanes]


def pack(store, target, span):
    for at, lanes in panels(span):
        height = store.shape[1] // ROWS
        target[:, :, lanes] = store[at].reshape(height, ROWS, LANES).astype(jnp.bfloat16)


def greet(groups):
    barrier = pltpu.get_barrier_semaphore()
    total = 0
    for axes, count in groups:
        me = position(axes)

        @pl.loop(1, count)
        def _(step):
            there = coordinates(axes, lax.rem(me + step, count))
            pl.semaphore_signal(barrier, inc=1, device_id=there, device_id_type=MESH)

        total += count - 1
    pl.semaphore_wait(barrier, total)


def standardize(source, plain):
    values = source.astype(jnp.float32)
    average = jnp.sum(values, axis=0) / values.shape[0]
    centred = values - average
    spread = jnp.sum(centred * centred, axis=0) / values.shape[0]
    result = centred * lax.rsqrt(spread + EPSILON)
    for at, lanes in panels(values.shape[2]):
        plain[at] = result[:, :, lanes].reshape(plain.shape[1:])


def front_kernel(
    flat, count, quads, pair, mask, gain, weights,
    wide_left, far_right, gate,
    landed, plain, sided, outgoing,
    pair_send, pair_recv, pair_own, sends, receives, gsend, greceive, own,
):
    me = position(flat)
    quad = lax.axis_index("gz")
    core = lax.axis_index("gy")
    cores = lax.axis_size("gy")
    chunks, channels, _, span = landed.shape
    local = pair.shape[0]
    rows = chunks * ROWS
    hidden = outgoing.shape[2]
    depth = hidden // count
    greet(((flat, count), (("gy",), cores)))
    columns = pl.ds(pl.multiple_of(core * span, span), span)

    def pair_copy(chunk, step, sender, target):
        first = pl.multiple_of(target * rows + chunk * ROWS, ROWS)
        return pltpu.make_async_remote_copy(
            src_ref=pair.at[:, pl.ds(first, ROWS), :],
            dst_ref=landed.at[chunk, pl.ds(sender * local, local)],
            send_sem=pair_send.at[chunk, step],
            recv_sem=pair_recv.at[chunk, step],
            device_id={"gz": target},
            device_id_type=MESH,
        )

    def pair_keep(chunk):
        first = pl.multiple_of(quad * rows + chunk * ROWS, ROWS)
        return pltpu.make_async_copy(
            pair.at[:, pl.ds(first, ROWS), :],
            landed.at[chunk, pl.ds(quad * local, local)],
            pair_own.at[chunk],
        )

    def landing(side, chunk, sender):
        cut = pl.ds(pl.multiple_of(chunk * ROWS, ROWS), ROWS)
        if side == 0:
            return wide_left.at[:, sender, cut, columns]
        return far_right.at[:, sender, cut, :]

    def copy(side, chunk, step, sender, target):
        return pltpu.make_async_remote_copy(
            src_ref=outgoing.at[side, chunk, pl.ds(target * depth, depth)],
            dst_ref=landing(side, chunk, sender),
            send_sem=sends.at[side, chunk, step],
            recv_sem=receives.at[side, chunk, step],
            device_id=coordinates(flat, target),
            device_id_type=MESH,
        )

    def keep(side, chunk):
        return pltpu.make_async_copy(
            outgoing.at[side, chunk, pl.ds(me * depth, depth)],
            landing(side, chunk, me),
            own.at[side, chunk],
        )

    def passed(chunk, ahead):
        cut = pl.ds(pl.multiple_of(chunk * ROWS, ROWS), ROWS)
        return pltpu.make_async_remote_copy(
            src_ref=wide_left.at[:, :, cut, columns],
            dst_ref=wide_left.at[:, :, cut, columns],
            send_sem=gsend.at[chunk, ahead],
            recv_sem=greceive.at[chunk, ahead],
            device_id={"gy": lax.rem(core + ahead, cores)},
            device_id_type=MESH,
        )

    @pl.loop(0, chunks)
    def _(chunk):
        pair_keep(chunk).start()

        @pl.loop(1, quads)
        def _(step):
            pair_copy(chunk, step, quad, lax.rem(quad + step, quads)).start()

    @pl.loop(0, chunks)
    def _(chunk):
        @pl.loop(1, quads)
        def _(step):
            pair_copy(
                chunk, step, lax.rem(quad - step + quads, quads), lax.rem(quad + step, quads)
            ).wait()

        pair_keep(chunk).wait()
        standardize(landed[chunk], plain)

        @pl.loop(0, ROWS)
        def _(row):
            normed = (row_of(plain, row, channels, span) * gain[...]).astype(jnp.bfloat16)
            inside = mask[pl.ds(chunk * ROWS + row, 1), :]

            def product(at):
                return jnp.dot(weights[at], normed, preferred_element_type=jnp.float32)

            for side in range(2):
                gated = inside * jax.nn.sigmoid(product(2 * side)) * product(2 * side + 1)
                put_row(sided.at[side], row, hidden, span, gated)
            gate[chunk * ROWS + row] = jax.nn.sigmoid(product(4))

        for side in range(2):
            pack(sided.at[side], outgoing.at[side, chunk], span)

        for side in range(2):
            @pl.loop(1, count)
            def _(step):
                copy(side, chunk, step, me, lax.rem(me + step, count)).start()

            keep(side, chunk).start()

    @pl.loop(0, chunks)
    def _(chunk):
        for side in range(2):
            @pl.loop(1, count)
            def _(step):
                copy(
                    side, chunk, step, lax.rem(me - step + count, count), lax.rem(me + step, count)
                ).wait()

            keep(side, chunk).wait()
            if side == 0:
                for ahead in range(1, cores):
                    passed(chunk, ahead).start()

    @pl.loop(0, chunks)
    def _(chunk):
        for ahead in range(1, cores):
            passed(chunk, ahead).wait()


def back_kernel(
    flat, count, quads, wide_left, far_right, gate, mask, gain, weights,
    update,
    triangle, landed, plain, sided, outgoing,
    sends, receives, out_send, out_recv, out_own,
):
    me = position(flat)
    quad = lax.axis_index("gz")
    chunks, hidden, _, span = landed.shape
    channels = outgoing.shape[1]
    local = channels // quads
    rows = chunks * ROWS
    depth = hidden // count
    greet(((flat, count),))

    def copy(chunk, step, sender, target):
        return pltpu.make_async_remote_copy(
            src_ref=triangle.at[:, target, chunk],
            dst_ref=landed.at[chunk, pl.ds(sender * depth, depth)],
            send_sem=sends.at[chunk, step],
            recv_sem=receives.at[chunk, step],
            device_id=coordinates(flat, target),
            device_id_type=MESH,
        )

    def out_copy(chunk, step, sender, target):
        first = pl.multiple_of(sender * rows + chunk * ROWS, ROWS)
        return pltpu.make_async_remote_copy(
            src_ref=outgoing.at[chunk, pl.ds(target * local, local)],
            dst_ref=update.at[:, pl.ds(first, ROWS), :],
            send_sem=out_send.at[chunk, step],
            recv_sem=out_recv.at[chunk, step],
            device_id={"gz": target},
            device_id_type=MESH,
        )

    def out_keep(chunk):
        first = pl.multiple_of(quad * rows + chunk * ROWS, ROWS)
        return pltpu.make_async_copy(
            outgoing.at[chunk, pl.ds(quad * local, local)],
            update.at[:, pl.ds(first, ROWS), :],
            out_own.at[chunk],
        )

    @pl.loop(0, depth)
    def _(at):
        product = lax.dot_general(
            wide_left[at], far_right[at], (((0,), (0,)), ((), ())),
            preferred_element_type=jnp.float32,
        )
        triangle[at] = product.reshape(count, chunks, ROWS, span).astype(jnp.bfloat16)

    @pl.loop(0, chunks)
    def _(chunk):
        @pl.loop(1, count)
        def _(step):
            copy(chunk, step, me, lax.rem(me + step, count)).start()

    @pl.loop(0, chunks)
    def _(chunk):
        @pl.loop(0, depth)
        def _(at):
            landed[chunk, me * depth + at] = triangle[at, me, chunk]

        @pl.loop(1, count)
        def _(step):
            copy(
                chunk, step, lax.rem(me - step + count, count), lax.rem(me + step, count)
            ).wait()

        standardize(landed[chunk], plain)

        @pl.loop(0, ROWS)
        def _(row):
            normed = (row_of(plain, row, hidden, span) * gain[...]).astype(jnp.bfloat16)
            inside = mask[pl.ds(chunk * ROWS + row, 1), :]
            projected = jnp.dot(weights[...], normed, preferred_element_type=jnp.float32)
            gated = inside * gate[chunk * ROWS + row] * projected
            put_row(sided, row, channels, span, gated)

        pack(sided, outgoing.at[chunk], span)

        @pl.loop(1, quads)
        def _(step):
            out_copy(chunk, step, quad, lax.rem(quad + step, quads)).start()

        out_keep(chunk).start()

    @pl.loop(0, chunks)
    def _(chunk):
        @pl.loop(1, quads)
        def _(step):
            out_copy(
                chunk, step, lax.rem(quad - step + quads, quads), lax.rem(quad + step, quads)
            ).wait()

        out_keep(chunk).wait()


def shards(pair, pair_mask, input_gain, input_weights, out_gate_weight, hidden_gain, out_weight):
    flat = ("gx", "gz")
    quads = lax.axis_size("gz")
    count = lax.axis_size("gx") * quads
    cores = lax.axis_size("gy")
    local, tall, span = pair.shape
    rows = tall // quads
    chunks = rows // ROWS
    channels = input_gain.shape[0]
    hidden = hidden_gain.shape[0]
    depth = hidden // count
    own_mask = lax.dynamic_slice_in_dim(pair_mask, lax.axis_index("gz") * rows, rows, 0)
    mask_values = own_mask.astype(jnp.float32)
    turned = jnp.concatenate(
        [jnp.swapaxes(input_weights, 1, 2), jnp.swapaxes(out_gate_weight, 0, 1)[None]], axis=0
    )
    wide_gain = jnp.broadcast_to(input_gain[:, None], (channels, span))
    wide_hidden = jnp.broadcast_to(hidden_gain[:, None], (hidden, span))
    near = pl.BlockSpec(memory_space=pltpu.VMEM)
    far = pl.BlockSpec(memory_space=pl.ANY)
    copies = pltpu.SemaphoreType.DMA
    wide_left, far_right, gate = pl.pallas_call(
        functools.partial(front_kernel, flat, count, quads),
        out_shape=(
            jax.ShapeDtypeStruct((depth, count, rows, span * cores), jnp.bfloat16),
            jax.ShapeDtypeStruct((depth, count, rows, span), jnp.bfloat16),
            jax.ShapeDtypeStruct((rows, channels, span), jnp.float32),
        ),
        in_specs=[far, near, near, near],
        out_specs=(far, far, near),
        scratch_shapes=[
            pltpu.VMEM((chunks, channels, ROWS, span), jnp.bfloat16),
            pltpu.VMEM((span // LANES, channels * ROWS, LANES), jnp.float32),
            pltpu.VMEM((2, span // LANES, hidden * ROWS, LANES), jnp.float32),
            pltpu.VMEM((2, chunks, hidden, ROWS, span), jnp.bfloat16),
            copies((chunks, quads)),
            copies((chunks, quads)),
            copies((chunks,)),
            copies((2, chunks, count)),
            copies((2, chunks, count)),
            copies((chunks, cores)),
            copies((chunks, cores)),
            copies((2, chunks)),
        ],
        compiler_params=pltpu.CompilerParams(
            collective_id=0, has_side_effects=True, vmem_limit_bytes=40 << 20
        ),
    )(pair, mask_values, wide_gain, turned)
    return pl.pallas_call(
        functools.partial(back_kernel, flat, count, quads),
        out_shape=jax.ShapeDtypeStruct(pair.shape, jnp.bfloat16),
        in_specs=[near] * 6,
        out_specs=far,
        scratch_shapes=[
            pltpu.VMEM((depth, count, chunks, ROWS, span), jnp.bfloat16),
            pltpu.VMEM((chunks, hidden, ROWS, span), jnp.bfloat16),
            pltpu.VMEM((span // LANES, hidden * ROWS, LANES), jnp.float32),
            pltpu.VMEM((span // LANES, channels * ROWS, LANES), jnp.float32),
            pltpu.VMEM((chunks, channels, ROWS, span), jnp.bfloat16),
            copies((chunks, count)),
            copies((chunks, count)),
            copies((chunks, quads)),
            copies((chunks, quads)),
            copies((chunks,)),
        ],
        compiler_params=pltpu.CompilerParams(
            collective_id=1, has_side_effects=True, vmem_limit_bytes=48 << 20
        ),
    )(
        wide_left.reshape(depth, count * rows, span * cores),
        far_right.reshape(depth, count * rows, span),
        gate,
        mask_values,
        wide_hidden,
        jnp.swapaxes(out_weight, 0, 1),
    )


def solution(mesh):
    placed = (P("gz", "gx", "gy"), P("gx", "gy"), P(), P(), P(), P(), P())
    return jax.shard_map(
        shards, mesh=mesh, in_specs=placed, out_specs=P("gz", "gx", "gy"), check_vma=False
    )
```

time: 594 us -> 190 us (0.32)
  waiting for transfers between devices: 290 us -> 0 us
  blocking collectives: 207 us -> 0 us
  Pallas kernels: 0 us -> 177 us
  matrix products: 37.5 us -> 0 us
  other arithmetic: 16.8 us -> 0.78 us
  local copies, waits for them, and re-layouts: 26.2 us -> 11 us
  between operations: 13.6 us -> 0.08 us
    all_to_all x1 -> x0, blocking collectives: 207 us -> none  [shards(): lax.all_to_all(left_panels, 'gx', split_axis=2, concat_axis=1, tiled=True)]
    all_gather x4 -> x0, waiting for transfers between devices: 202 us -> none  [the longest x1 87.6 us: shards(): every_hidden = lax.all_gather(hidden_normed, 'gz', axis=1, tiled=True)]
    pallas_call x0 -> x2, Pallas kernels: none -> 177 us  [the longest x1 109 us: shards(): pl.pallas_call(functools.partial(front_kernel, flat, count, quads), out_s...]
    psum x2 -> x0, waiting for transfers between devices: 87.2 us -> none  [the longest x1 43.9 us: shards(): lax.psum((jnp.sum(triangle, axis=1), jnp.sum(triangle * triangle, axis=1)...]
    dot_general x5 -> x0, matrix products: 37.5 us -> none  [the longest x1 17.5 us: shards(): jnp.einsum('cki,ckj->icj', row_blocks, lax.all_gather(right_side, 'gx', a...]
    convert_element_type x4 -> x1, other arithmetic: 10 us -> 0.76 us  [shards(): mask_values = own_mask.astype(jnp.float32)]
    all_gather x1 -> x0, local copies, waits for them, and re-layouts: 9.18 us -> none  [shards(): left_panels = lax.all_gather(left_side, 'gy', axis=2, tiled=True)]
    unnamed x20 -> x10, local copies, waits for them, and re-layouts: 1.4 us -> 9.57 us
  transfers between devices with their start and end apart: 6 -> 0, of which waited for: 6 -> 0; matrix products, arithmetic and copies ran while one was open for 3% -> 0% of each run, Pallas kernels for 0% -> 0%
where the time goes in v2:
time: 190 us; the launch traced here: 189 us
  Pallas kernels  177 us (93%)
  local copies, waits for them, and re-layouts  11 us (6%)
    pallas_call x1, Pallas kernels, shards(): pl.pallas_call(functools.partial(front_kernel, flat, count, quads), out_s...  109 us
    pallas_call x1, Pallas kernels, shards(): pl.pallas_call(functools.partial(back_kernel, flat, count, quads), out_sh...  67.9 us
    unnamed x10, local copies, waits for them, and re-layouts  9.57 us

profile of v2, /device:TPU:26, one launch (start us, length us, event | category | flops | bytes accessed | tf_op | source)
XLA Modules:
  0.0 188.9 jit_solution(3362100139357061742)
XLA Ops:
  0.0 0.8 dynamic-slice_convert_fusion.mask
  0.8 0.9 copy.9
  1.6 0.9 copy.10
  2.5 0.7 broadcast_in_dim.6.gain
  3.3 1.0 copy.8
  4.3 0.7 broadcast_in_dim.8.gain
  5.1 0.0 copy-start.2
  5.1 1.6 copy-done.2
  6.6 109.2 %shard_map.73 = (bf16[8,16,32,512]{3,2,1,0:T(8,128)(2,1)S(1)}, bf16[8,16,32,256]{3,2,1,0:T(8,128)(2,1)S(1)}, f32[32,128,256]{2,1,0:T(8,128)S(1)}) custom-call(bf16[32,128,256]{2,1,0:T(8,128)(2,1)S(1)} %copy-done.2, f32[32,256]{1,0:T(8,128)S(1)} %dynamic-slice_convert_fusion.mask, f32[128,256]{1,0:T(8,128)S(1)} %broadcast_in_dim.6.gain, ...), custom_call_target="tpu_custom_call" | custom-call | tf_op jit(solution)/shard_map/pallas_call | solution.py:331
  115.8 0.0 copy-start
  115.8 1.9 %copy-done = bf16[8,16,32,512]{3,2,1,0:T(8,128)(2,1)} copy-done((bf16[8,16,32,512]{3,2,1,0:T(8,128)(2,1)}, bf16[8,16,32,512]{3,2,1,0:T(8,128)(2,1)S(1)}, u32[]{:S(2)}) %copy-start) | copy-done | bytes 4194328
  117.8 0.0 copy-start.1
  117.8 2.0 %copy-done.1 = f32[32,128,256]{2,1,0:T(8,128)} copy-done((f32[32,128,256]{2,1,0:T(8,128)}, f32[32,128,256]{2,1,0:T(8,128)S(1)}, u32[]{:S(2)}) %copy-start.1) | copy-done | bytes 4194328
  119.7 67.9 %shard_map.74 = bf16[32,128,256]{2,1,0:T(8,128)(2,1)S(1)} custom-call(bf16[8,512,512]{2,1,0:T(8,128)(2,1)} %bitcast.7, bf16[8,512,256]{2,1,0:T(8,128)(2,1)S(1)} %bitcast.8, f32[32,128,256]{2,1,0:T(8,128)} %copy-done.1, f32[32,256]{1,0:T(8,128)S(1)} %dynamic-slice_convert_fusion.mask, f32[128,256]{1,0:T(8,128)S(1)} %broadcast_in_dim.8.gain, ...), custom_call_target="tpu_custom_call" | custom-call | tf_op jit(solution)/shard_map/pallas_call | solution.py:358
  187.6 1.3 copy.12
  (1 shorter events, 0.0 us)
Async XLA Ops:
  5.1 1.6 copy-start.2
  115.8 1.9 %copy-start = (bf16[8,16,32,512]{3,2,1,0:T(8,128)(2,1)}, bf16[8,16,32,512]{3,2,1,0:T(8,128)(2,1)S(1)}, u32[]{:S(2)}) copy-start(bf16[8,16,32,512]{3,2,1,0:T(8,128)(2,1)S(1)} %get-tuple-element.8) | copy-start | bytes 12582916
  117.8 2.0 %copy-start.1 = (f32[32,128,256]{2,1,0:T(8,128)}, f32[32,128,256]{2,1,0:T(8,128)S(1)}, u32[]{:S(2)}) copy-start(f32[32,128,256]{2,1,0:T(8,128)S(1)} %get-tuple-element.10.gate) | copy-start | bytes 12582916

commit v3 on v2

--- a/solution.py
+++ b/solution.py
@@ -75,11 +75,13 @@
         plain[at] = result[:, :, lanes].reshape(plain.shape[1:])
 
 
-def front_kernel(
-    flat, count, quads, pair, mask, gain, weights,
-    wide_left, far_right, gate,
-    landed, plain, sided, outgoing,
+def whole_kernel(
+    flat, count, quads, pair, mask, input_gain, input_weights, out_gate_weight, hidden_gain, out_weight,
+    update,
+    turned, spread_gain, wide_left, far_right, gate, triangle,
+    landed, plain, sided, outgoing, returned, finished,
     pair_send, pair_recv, pair_own, sends, receives, gsend, greceive, own,
+    back_send, back_recv, out_send, out_recv, out_own,
 ):
     me = position(flat)
     quad = lax.axis_index("gz")
@@ -89,8 +91,17 @@
     local = pair.shape[0]
     rows = chunks * ROWS
     hidden = outgoing.shape[2]
+    channels = landed.shape[1]
     depth = hidden // count
     greet(((flat, count), (("gy",), cores)))
+
+    def wide_gain(at):
+        return jnp.concatenate([spread_gain[at]] * (span // LANES), axis=1)
+
+    def inside_of(chunk, row):
+        first = quad * rows + chunk * ROWS + row
+        return mask[pl.ds(first, 1), :].astype(jnp.float32)
+
     columns = pl.ds(pl.multiple_of(core * span, span), span)
 
     def pair_copy(chunk, step, sender, target):
@@ -154,6 +165,13 @@
         def _(step):
             pair_copy(chunk, step, quad, lax.rem(quad + step, quads)).start()
 
+    for at in range(4):
+        turned[at] = input_weights[at].astype(jnp.float32).T.astype(jnp.bfloat16)
+    turned[4] = out_gate_weight[...].astype(jnp.float32).T.astype(jnp.bfloat16)
+    turned[5] = out_weight[...].astype(jnp.float32).T.astype(jnp.bfloat16)
+    spread_gain[0] = jnp.broadcast_to(input_gain[...], (LANES, channels)).T
+    spread_gain[1] = jnp.broadcast_to(hidden_gain[...], (LANES, hidden)).T
+
     @pl.loop(0, chunks)
     def _(chunk):
         @pl.loop(1, quads)
@@ -167,11 +185,11 @@
 
         @pl.loop(0, ROWS)
         def _(row):
-            normed = (row_of(plain, row, channels, span) * gain[...]).astype(jnp.bfloat16)
-            inside = mask[pl.ds(chunk * ROWS + row, 1), :]
+            normed = (row_of(plain, row, channels, span) * wide_gain(0)).astype(jnp.bfloat16)
+            inside = inside_of(chunk, row)
 
             def product(at):
-                return jnp.dot(weights[at], normed, preferred_element_type=jnp.float32)
+                return jnp.dot(turned[at], normed, preferred_element_type=jnp.float32)
 
             for side in range(2):
                 gated = inside * jax.nn.sigmoid(product(2 * side)) * product(2 * side + 1)
@@ -207,28 +225,12 @@
         for ahead in range(1, cores):
             passed(chunk, ahead).wait()
 
-
-def back_kernel(
-    flat, count, quads, wide_left, far_right, gate, mask, gain, weights,
-    update,
-    triangle, landed, plain, sided, outgoing,
-    sends, receives, out_send, out_recv, out_own,
-):
-    me = position(flat)
-    quad = lax.axis_index("gz")
-    chunks, hidden, _, span = landed.shape
-    channels = outgoing.shape[1]
-    local = channels // quads
-    rows = chunks * ROWS
-    depth = hidden // count
-    greet(((flat, count),))
-
-    def copy(chunk, step, sender, target):
+    def back_copy(chunk, step, sender, target):
         return pltpu.make_async_remote_copy(
             src_ref=triangle.at[:, target, chunk],
-            dst_ref=landed.at[chunk, pl.ds(sender * depth, depth)],
-            send_sem=sends.at[chunk, step],
-            recv_sem=receives.at[chunk, step],
+            dst_ref=returned.at[chunk, pl.ds(sender * depth, depth)],
+            send_sem=back_send.at[chunk, step],
+            recv_sem=back_recv.at[chunk, step],
             device_id=coordinates(flat, target),
             device_id_type=MESH,
         )
@@ -236,7 +238,7 @@
     def out_copy(chunk, step, sender, target):
         first = pl.multiple_of(sender * rows + chunk * ROWS, ROWS)
         return pltpu.make_async_remote_copy(
-            src_ref=outgoing.at[chunk, pl.ds(target * local, local)],
+            src_ref=finished.at[chunk, pl.ds(target * local, local)],
             dst_ref=update.at[:, pl.ds(first, ROWS), :],
             send_sem=out_send.at[chunk, step],
             recv_sem=out_recv.at[chunk, step],
@@ -247,7 +249,7 @@
     def out_keep(chunk):
         first = pl.multiple_of(quad * rows + chunk * ROWS, ROWS)
         return pltpu.make_async_copy(
-            outgoing.at[chunk, pl.ds(quad * local, local)],
+            finished.at[chunk, pl.ds(quad * local, local)],
             update.at[:, pl.ds(first, ROWS), :],
             out_own.at[chunk],
         )
@@ -255,7 +257,8 @@
     @pl.loop(0, depth)
     def _(at):
         product = lax.dot_general(
-            wide_left[at], far_right[at], (((0,), (0,)), ((), ())),
+            wide_left[at].reshape(count * rows, -1),
+            far_right[at].reshape(count * rows, -1), (((0,), (0,)), ((), ())),
             preferred_element_type=jnp.float32,
         )
         triangle[at] = product.reshape(count, chunks, ROWS, span).astype(jnp.bfloat16)
@@ -264,31 +267,31 @@
     def _(chunk):
         @pl.loop(1, count)
         def _(step):
-            copy(chunk, step, me, lax.rem(me + step, count)).start()
+            back_copy(chunk, step, me, lax.rem(me + step, count)).start()
 
     @pl.loop(0, chunks)
     def _(chunk):
         @pl.loop(0, depth)
         def _(at):
-            landed[chunk, me * depth + at] = triangle[at, me, chunk]
+            returned[chunk, me * depth + at] = triangle[at, me, chunk]
 
         @pl.loop(1, count)
         def _(step):
-            copy(
+            back_copy(
                 chunk, step, lax.rem(me - step + count, count), lax.rem(me + step, count)
             ).wait()
 
-        standardize(landed[chunk], plain)
+        standardize(returned[chunk], plain)
 
         @pl.loop(0, ROWS)
         def _(row):
-            normed = (row_of(plain, row, hidden, span) * gain[...]).astype(jnp.bfloat16)
-            inside = mask[pl.ds(chunk * ROWS + row, 1), :]
-            projected = jnp.dot(weights[...], normed, preferred_element_type=jnp.float32)
+            normed = (row_of(plain, row, hidden, span) * wide_gain(1)).astype(jnp.bfloat16)
+            inside = inside_of(chunk, row)
+            projected = jnp.dot(turned[5], normed, preferred_element_type=jnp.float32)
             gated = inside * gate[chunk * ROWS + row] * projected
-            put_row(sided, row, channels, span, gated)
-
-        pack(sided, outgoing.at[chunk], span)
+            put_row(sided.at[0], row, channels, span, gated)
+
+        pack(sided.at[0], finished.at[chunk], span)
 
         @pl.loop(1, quads)
         def _(step):
@@ -318,30 +321,29 @@
     channels = input_gain.shape[0]
     hidden = hidden_gain.shape[0]
     depth = hidden // count
-    own_mask = lax.dynamic_slice_in_dim(pair_mask, lax.axis_index("gz") * rows, rows, 0)
-    mask_values = own_mask.astype(jnp.float32)
-    turned = jnp.concatenate(
-        [jnp.swapaxes(input_weights, 1, 2), jnp.swapaxes(out_gate_weight, 0, 1)[None]], axis=0
-    )
-    wide_gain = jnp.broadcast_to(input_gain[:, None], (channels, span))
-    wide_hidden = jnp.broadcast_to(hidden_gain[:, None], (hidden, span))
     near = pl.BlockSpec(memory_space=pltpu.VMEM)
     far = pl.BlockSpec(memory_space=pl.ANY)
     copies = pltpu.SemaphoreType.DMA
-    wide_left, far_right, gate = pl.pallas_call(
-        functools.partial(front_kernel, flat, count, quads),
-        out_shape=(
-            jax.ShapeDtypeStruct((depth, count, rows, span * cores), jnp.bfloat16),
-            jax.ShapeDtypeStruct((depth, count, rows, span), jnp.bfloat16),
-            jax.ShapeDtypeStruct((rows, channels, span), jnp.float32),
-        ),
-        in_specs=[far, near, near, near],
-        out_specs=(far, far, near),
+    tiles = span // LANES
+    tallest = max(channels, hidden)
+    return pl.pallas_call(
+        functools.partial(whole_kernel, flat, count, quads),
+        out_shape=jax.ShapeDtypeStruct(pair.shape, jnp.bfloat16),
+        in_specs=[far] + [near] * 6,
+        out_specs=far,
         scratch_shapes=[
+            pltpu.VMEM((6, tallest, tallest), jnp.bfloat16),
+            pltpu.VMEM((2, tallest, LANES), jnp.float32),
+            pltpu.VMEM((depth, count, rows, span * cores), jnp.bfloat16),
+            pltpu.VMEM((depth, count, rows, span), jnp.bfloat16),
+            pltpu.VMEM((rows, channels, span), jnp.float32),
+            pltpu.VMEM((depth, count, chunks, ROWS, span), jnp.bfloat16),
             pltpu.VMEM((chunks, channels, ROWS, span), jnp.bfloat16),
-            pltpu.VMEM((span // LANES, channels * ROWS, LANES), jnp.float32),
-            pltpu.VMEM((2, span // LANES, hidden * ROWS, LANES), jnp.float32),
+            pltpu.VMEM((tiles, tallest * ROWS, LANES), jnp.float32),
+            pltpu.VMEM((2, tiles, tallest * ROWS, LANES), jnp.float32),
             pltpu.VMEM((2, chunks, hidden, ROWS, span), jnp.bfloat16),
+            pltpu.VMEM((chunks, hidden, ROWS, span), jnp.bfloat16),
+            pltpu.VMEM((chunks, channels, ROWS, span), jnp.bfloat16),
             copies((chunks, quads)),
             copies((chunks, quads)),
             copies((chunks,)),
@@ -350,22 +352,6 @@
             copies((chunks, cores)),
             copies((chunks, cores)),
             copies((2, chunks)),
-        ],
-        compiler_params=pltpu.CompilerParams(
-            collective_id=0, has_side_effects=True, vmem_limit_bytes=40 << 20
-        ),
-    )(pair, mask_values, wide_gain, turned)
-    return pl.pallas_call(
-        functools.partial(back_kernel, flat, count, quads),
-        out_shape=jax.ShapeDtypeStruct(pair.shape, jnp.bfloat16),
-        in_specs=[near] * 6,
-        out_specs=far,
-        scratch_shapes=[
-            pltpu.VMEM((depth, count, chunks, ROWS, span), jnp.bfloat16),
-            pltpu.VMEM((chunks, hidden, ROWS, span), jnp.bfloat16),
-            pltpu.VMEM((span // LANES, hidden * ROWS, LANES), jnp.float32),
-            pltpu.VMEM((span // LANES, channels * ROWS, LANES), jnp.float32),
-            pltpu.VMEM((chunks, channels, ROWS, span), jnp.bfloat16),
             copies((chunks, count)),
             copies((chunks, count)),
             copies((chunks, quads)),
@@ -373,15 +359,16 @@
             copies((chunks,)),
         ],
         compiler_params=pltpu.CompilerParams(
-            collective_id=1, has_side_effects=True, vmem_limit_bytes=48 << 20
+            collective_id=0, has_side_effects=True, vmem_limit_bytes=60 << 20
         ),
     )(
-        wide_left.reshape(depth, count * rows, span * cores),
-        far_right.reshape(depth, count * rows, span),
-        gate,
-        mask_values,
-        wide_hidden,
-        jnp.swapaxes(out_weight, 0, 1),
+        pair,
+        pair_mask,
+        input_gain[None],
+        input_weights,
+        out_gate_weight,
+        hidden_gain[None],
+        out_weight,
     )
 
 

time: 190 us -> 176 us (0.926)
  local copies, waits for them, and re-layouts: 11 us -> 3.13 us
  Pallas kernels: 177 us -> 173 us
    unnamed x10 -> x1, local copies, waits for them, and re-layouts: 9.57 us -> 3.13 us
    pallas_call x2 -> x1, Pallas kernels: 177 us -> 173 us  [shards(): pl.pallas_call(functools.partial(whole_kernel, flat, count, quads), out_s...]
where the time goes in v3:
time: 176 us
  Pallas kernels  173 us (98%)
  local copies, waits for them, and re-layouts  3.13 us (2%)
    pallas_call x1, Pallas kernels, shards(): pl.pallas_call(functools.partial(whole_kernel, flat, count, quads), out_s...  173 us

profile of v3, /device:TPU:26, one launch (start us, length us, event | category | flops | bytes accessed | tf_op | source)
XLA Modules:
  0.0 176.3 jit_solution(15355293917763658035)
XLA Ops:
  0.0 173.1 %shard_map.73 = bf16[32,128,256]{2,1,0:T(8,128)(2,1)} custom-call(bf16[32,128,256]{2,1,0:T(8,128)(2,1)} %pair.1, s32[128,256]{1,0:T(8,128)} %mask.1, f32[1,128]{1,0:T(1,128)} %bitcast.2, bf16[4,128,128]{2,1,0:T(8,128)(2,1)} %input_weights.1, bf16[128,128]{1,0:T(8,128)(2,1)} %out_gate_weight.1, f32[1,128]{1,0:T(1,128)} %bitcast.3, bf16[128,128]{1,0:T(8,128)(2,1)} %out_weight.1), custom_call_target="tpu_custom_call" | custom-call | tf_op jit(solution)/shard_map/pallas_call | solution.py:329
  173.2 3.1 %copy.9 = bf16[32,128,256]{2,1,0:T(8,128)(2,1)} copy(bf16[32,128,256]{2,1,0:T(8,128)(2,1)} %shard_map.73) | data formatting | bytes 4194304

commit v4 on v3

--- a/solution.py
+++ b/solution.py
@@ -183,28 +183,30 @@
         pair_keep(chunk).wait()
         standardize(landed[chunk], plain)
 
-        @pl.loop(0, ROWS)
-        def _(row):
-            normed = (row_of(plain, row, channels, span) * wide_gain(0)).astype(jnp.bfloat16)
-            inside = inside_of(chunk, row)
-
-            def product(at):
-                return jnp.dot(turned[at], normed, preferred_element_type=jnp.float32)
-
-            for side in range(2):
-                gated = inside * jax.nn.sigmoid(product(2 * side)) * product(2 * side + 1)
-                put_row(sided.at[side], row, hidden, span, gated)
-            gate[chunk * ROWS + row] = jax.nn.sigmoid(product(4))
+        def normed_row(row):
+            return (row_of(plain, row, channels, span) * wide_gain(0)).astype(jnp.bfloat16)
+
+        def product(at, normed):
+            return jnp.dot(turned[at], normed, preferred_element_type=jnp.float32)
 
         for side in range(2):
+            @pl.loop(0, ROWS)
+            def _(row):
+                normed = normed_row(row)
+                gating = inside_of(chunk, row) * jax.nn.sigmoid(product(2 * side, normed))
+                put_row(sided.at[side], row, hidden, span, gating * product(2 * side + 1, normed))
+
             pack(sided.at[side], outgoing.at[side, chunk], span)
 
-        for side in range(2):
             @pl.loop(1, count)
             def _(step):
                 copy(side, chunk, step, me, lax.rem(me + step, count)).start()
 
             keep(side, chunk).start()
+
+        @pl.loop(0, ROWS)
+        def _(row):
+            gate[chunk * ROWS + row] = jax.nn.sigmoid(product(4, normed_row(row)))
 
     @pl.loop(0, chunks)
     def _(chunk):

time: 176 us -> 176 us (level)
  no operation moved by 1% of the time
where the time goes in v4:
time: 176 us
  Pallas kernels  173 us (98%)
  local copies, waits for them, and re-layouts  3.13 us (2%)
    pallas_call x1, Pallas kernels, shards(): pl.pallas_call(functools.partial(whole_kernel, flat, count, quads), out_s...  173 us

profile of v4, /device:TPU:26, one launch (start us, length us, event | category | flops | bytes accessed | tf_op | source)
XLA Modules:
  0.0 175.7 jit_solution(10749553355866019031)
XLA Ops:
  0.0 172.6 %shard_map.73 = bf16[32,128,256]{2,1,0:T(8,128)(2,1)} custom-call(bf16[32,128,256]{2,1,0:T(8,128)(2,1)} %pair.1, s32[128,256]{1,0:T(8,128)} %mask.1, f32[1,128]{1,0:T(1,128)} %bitcast.2, bf16[4,128,128]{2,1,0:T(8,128)(2,1)} %input_weights.1, bf16[128,128]{1,0:T(8,128)(2,1)} %out_gate_weight.1, f32[1,128]{1,0:T(1,128)} %bitcast.3, bf16[128,128]{1,0:T(8,128)(2,1)} %out_weight.1), custom_call_target="tpu_custom_call" | custom-call | tf_op jit(solution)/shard_map/pallas_call | solution.py:331
  172.6 3.1 %copy.9 = bf16[32,128,256]{2,1,0:T(8,128)(2,1)} copy(bf16[32,128,256]{2,1,0:T(8,128)(2,1)} %shard_map.73) | data formatting | bytes 4194304
